TPU v7x, 32 devices: a whole 2x2x4 slice. The times are simulated.
32 devices in a mesh: gy: 2 (over y), gx: 4 (over z), gz: 4 (over x, core).
Axes of the slice: x: 2, y: 2, z: 4, core: 2. Of those that a mesh axis runs over, the one named last changes fastest.
Arguments:
- potential_warmth: float32 [32, 256, 512], P('gz', 'gy', 'gx'), may hold values from -6 to 6
- saltiness_anomaly: float32 [32, 256, 512], P('gz', 'gy', 'gx'), may hold values from -6 to 6
- squared_brunt_vaisala: float32 [32, 256, 512], P('gz', 'gy', 'gx'), may hold values from 0.5 to 2
- cross_density_mixing: float32 [32, 256, 512], P('gz', 'gy', 'gx'), may hold values from 0.1 to 10
- along_neutral_mixing: float32 [32, 256, 512], P('gz', 'gy', 'gx'), may hold values from 0.04 to 0.2
- layer_depth_mixing: float32 [32, 256, 512], P('gz', 'gy', 'gx'), may hold values from 0.04 to 0.2
- seawater_profile_flag: int32 [256, 512], P('gy', 'gx'), may hold values 0 or 1
- submerged_layer_total: int32 [256, 512], P('gy', 'gx'), may hold values from 1 to 32
Outputs:
- temperature_new: float32 [32, 256, 512], P('gz', 'gy', 'gx')
- salinity_new: float32 [32, 256, 512], P('gz', 'gy', 'gx')
All inputs are finite; a program needn't handle non-finite values. No bound on the sum of `seawater_profile_flag` on one device may be relied on, other than what follows from the above.
Results may differ from a plain program's by a relative error of at most 0.00002.
Values sent between devices are 32-bit elements; how exact they have to be, the bound alone decides.
A program may use at most 128 MiB of HBM per device.

v0:
```python
import functools

import jax
import jax.numpy as jnp
from jax import lax
from jax.experimental import pallas as pl
from jax.experimental.pallas import tpu as pltpu
from jax.sharding import PartitionSpec as P

MESH = pl.DeviceIdType.MESH
CHUNK = 16
PAD = 8
ORIG, LATE = 5, 3
(Z_UP, Z_DOWN, V_DOWN, PRE, XA_R, XA_L, YA_L, YA_R, XB_R, XB_L, YB_L, YB_R, PROD_UP, PROD_DOWN, CHAIN, MIDDLE, BACK) = range(17)


def kernel(
    t_in, s_in, n_in, v_in, i_in, g_in, flag_in, count_in,
    t_out, s_out,
    ext, late, depth, zh, vext, flag, count, psend, pre,
    xa, xa_got, xb, xb_got, ya, ya_got, yb, yb_got, comb_a, comb_b,
    prod, rhs, cpl, elim, ch_out, ch_in, mid_in, last, solved, back_in,
    local_sem, send_sem, recv_sem,
):
    L, R, C = t_in.shape
    gx, gy, gz = (lax.axis_index(a) for a in ("gx", "gy", "gz"))
    nx, ny, nz = (lax.axis_size(a) for a in ("gx", "gy", "gz"))
    right, left = lax.rem(gx + 1, nx), lax.rem(gx + nx - 1, nx)
    later, earlier = lax.rem(gy + 1, ny), lax.rem(gy + ny - 1, ny)
    below, above = lax.rem(gz + 1, nz), lax.rem(gz + nz - 1, nz)
    inner = pl.ds(PAD, R)
    f32 = jnp.float32

    def load(number, src, dst):
        return pltpu.make_async_copy(src, dst, local_sem.at[number])

    loads = [
        load(0, n_in, ext.at[:, 2, inner, :]),
        load(1, t_in, ext.at[:, 0, inner, :]),
        load(2, s_in, ext.at[:, 1, inner, :]),
        load(3, i_in, ext.at[:, 3, inner, :]),
        load(4, g_in, ext.at[:, 4, inner, :]),
        load(5, flag_in, flag),
        load(6, count_in, count),
        load(7, v_in, vext.at[pl.ds(1, L)]),
    ]
    for item in loads:
        item.start()

    barrier = pltpu.get_barrier_semaphore()
    for target in ({"gx": right}, {"gx": left}, {"gy": later}, {"gy": earlier}, {"gz": below}, {"gz": above}):
        pl.semaphore_signal(barrier, inc=1, device_id=target, device_id_type=MESH)
    pl.semaphore_wait(barrier, 6)

    def remote(number, src, dst, target):
        return pltpu.make_async_remote_copy(
            src_ref=src, dst_ref=dst, send_sem=send_sem.at[number], recv_sem=recv_sem.at[number],
            device_id=target, device_id_type=MESH,
        )

    has_above, has_below = gz > 0, gz < nz - 1
    has_earlier, has_later = gy > 0, gy < ny - 1
    always = None

    def when(condition, action):
        if condition is None:
            action()
        else:
            pl.when(condition)(action)

    sends = []

    def send(condition, item):
        when(condition, item.start)
        sends.append((condition, item))

    z_up = remote(Z_UP, ext.at[0, pl.ds(0, 2), inner, :], zh.at[1], {"gz": above})
    z_down = remote(Z_DOWN, ext.at[L - 1, pl.ds(0, 2), inner, :], zh.at[0], {"gz": below})
    v_down = remote(V_DOWN, vext.at[L], vext.at[0], {"gz": below})
    p_down = remote(PRE, psend, pre, {"gz": below})

    loads[0].wait()

    def column_sum(step, carry):
        rows = pl.ds(pl.multiple_of(step * CHUNK, PAD), CHUNK)
        rows_e = pl.ds(pl.multiple_of(PAD + step * CHUNK, PAD), CHUNK)
        total = ext[0, 2, rows_e, :]
        for k in range(1, L):
            total = total + ext[k, 2, rows_e, :]
        psend[rows, :] = total
        return carry

    chunks = R // CHUNK
    lax.fori_loop(0, chunks, column_sum, 0)

    @pl.when(gz == 0)
    def _():
        pre[...] = jnp.zeros_like(pre)

    @pl.when(gz == 0)
    def _():
        p_down.start()

    sends.append((has_below, p_down))
    loads[1].wait()
    loads[2].wait()
    send(has_above, z_up)
    send(has_below, z_down)

    loads[5].wait()
    loads[6].wait()
    depth[inner, :] = jnp.where(flag[...] == 1, count[...], 0).astype(f32)

    @pl.when(gz > 0)
    def _():
        p_down.wait_recv()

        @pl.when(has_below)
        def _():
            psend[...] = psend[...] + pre[...]
            p_down.start()

    loads[3].wait()
    loads[4].wait()

    def pack(source, fields, extra, out):
        def body(step, carry):
            rows = pl.ds(pl.multiple_of(step * CHUNK, PAD), CHUNK)
            rows_e = pl.ds(pl.multiple_of(PAD + step * CHUNK, PAD), CHUNK)
            pair = lax.broadcasted_iota(jnp.int32, (CHUNK, C), 1) // 2
            acc = jnp.zeros((CHUNK, C), f32)
            for m in range(L * fields + extra):
                slab = depth[rows_e, :] if m == L * fields else source[m // fields, m % fields, rows_e, :]
                acc = jnp.where(pair == m, pltpu.roll(slab, 2 * m + 1, 1), acc)
            out[rows, :] = acc
            return carry

        lax.fori_loop(0, chunks, body, 0)

    def pack_rows(source, fields, extra, out):
        for m in range(L * fields + extra):
            for side, row in ((0, PAD), (1, PAD + R - 1)):
                if m == L * fields:
                    out[side, pl.ds(m, 1), :] = depth[pl.ds(row, 1), :]
                else:
                    out[side, pl.ds(m, 1), :] = source[m // fields, m % fields, pl.ds(row, 1), :]

    def unpack_rows(source, fields, extra, got):
        for m in range(L * fields + extra):
            for side, row in ((0, PAD - 1), (1, PAD + R)):
                value = got[side, pl.ds(m, 1), :]
                if m == L * fields:
                    depth[pl.ds(row, 1), :] = value
                else:
                    source[m // fields, m % fields, pl.ds(row, 1), :] = value

    def combine(got, out):
        lane = lax.broadcasted_iota(jnp.int32, (R, C), 1)
        out[...] = jnp.where(lane % 2 == 0, pltpu.roll(got[1], C - 1, 1), pltpu.roll(got[0], 1, 1))

    pack_rows(ext, ORIG, 1, ya)
    pack(ext, ORIG, 1, xa)
    ya_l = remote(YA_L, ya.at[0], ya_got.at[1], {"gy": earlier})
    ya_r = remote(YA_R, ya.at[1], ya_got.at[0], {"gy": later})
    xa_r = remote(XA_R, xa, xa_got.at[0], {"gx": right})
    xa_l = remote(XA_L, xa, xa_got.at[1], {"gx": left})
    send(has_earlier, ya_l)
    send(has_later, ya_r)
    send(always, xa_r)
    send(always, xa_l)
    loads[7].wait()
    send(has_below, v_down)

    @pl.when(gz == 0)
    def _():
        zh[0] = jnp.zeros_like(zh[0])
        vext[0] = jnp.zeros_like(vext[0])
        prod[0] = jnp.zeros_like(prod[0])

    @pl.when(gz == nz - 1)
    def _():
        zh[1] = jnp.zeros_like(zh[1])
        prod[L + 1] = jnp.zeros_like(prod[L + 1])

    @pl.when(gy == 0)
    def _():
        ya_got[0] = jnp.zeros_like(ya_got[0])
        yb_got[0] = jnp.zeros_like(yb_got[0])

    @pl.when(gy == ny - 1)
    def _():
        ya_got[1] = jnp.zeros_like(ya_got[1])
        yb_got[1] = jnp.zeros_like(yb_got[1])

    when(has_above, z_down.wait_recv)
    when(has_below, z_up.wait_recv)

    def wet_at(deep, k):
        level = gz * L + k
        return ((deep > level.astype(f32)) & (level >= 0)).astype(f32)

    def vertical(step, carry):
        rows = pl.ds(pl.multiple_of(step * CHUNK, PAD), CHUNK)
        rows_e = pl.ds(pl.multiple_of(PAD + step * CHUNK, PAD), CHUNK)
        deep = depth[rows_e, :]
        total = pre[rows, :]
        w_here = wet_at(deep, 0)
        gate = wet_at(deep, -1) * w_here
        cells = [ext[0, c, rows_e, :] for c in range(2)]
        over = [(cells[c] - zh[0, c, rows, :]) * gate for c in range(2)]
        for k in range(L):
            total = total + ext[k, 2, rows_e, :]
            late[k, 0, rows_e, :] = total
            w_next = wet_at(deep, k + 1)
            gate = w_here * w_next
            for c in range(2):
                following = ext[k + 1, c, rows_e, :] if k + 1 < L else zh[1, c, rows, :]
                under = (following - cells[c]) * gate
                late[k, 1 + c, rows_e, :] = 0.5 * (under + over[c])
                cells[c], over[c] = following, under
            w_here = w_next
        return carry

    lax.fori_loop(0, chunks, vertical, 0)
    pack_rows(late, LATE, 0, yb)
    pack(late, LATE, 0, xb)
    yb_l = remote(YB_L, yb.at[0], yb_got.at[1], {"gy": earlier})
    yb_r = remote(YB_R, yb.at[1], yb_got.at[0], {"gy": later})
    xb_r = remote(XB_R, xb, xb_got.at[0], {"gx": right})
    xb_l = remote(XB_L, xb, xb_got.at[1], {"gx": left})
    send(has_earlier, yb_l)
    send(has_later, yb_r)
    send(always, xb_r)
    send(always, xb_l)

    when(has_earlier, ya_r.wait_recv)
    when(has_later, ya_l.wait_recv)
    unpack_rows(ext, ORIG, 1, ya_got)
    xa_r.wait_recv()
    xa_l.wait_recv()
    combine(xa_got, comb_a)
    when(has_earlier, yb_r.wait_recv)
    when(has_later, yb_l.wait_recv)
    unpack_rows(late, LATE, 0, yb_got)
    xb_r.wait_recv()
    xb_l.wait_recv()
    combine(xb_got, comb_b)

    def face(a, b):
        wet = a["w"] * b["w"]
        lift = (b["B"] - a["B"]) * wet
        slope = -lift / (0.5 * (a["N"] + b["N"]) + jnp.abs(lift) + 1.0 - wet)
        along = 0.5 * (a["I"] + b["I"])
        skew = (along - 0.5 * (a["G"] + b["G"])) * slope * 0.5
        steps, fluxes = [], []
        for c, g in (("T", "gT"), ("S", "gS")):
            step = (b[c] - a[c]) * wet
            steps.append(step)
            fluxes.append(-(along * step + skew * (a[g] + b[g])))
        return slope, steps, fluxes

    names_a, names_b = ("T", "S", "N", "I", "G"), ("B", "gT", "gS")

    def level_body(k):
        for chunk in range(chunks):
            r0 = chunk * CHUNK
            rows = pl.ds(r0, CHUNK)
            lane = lax.broadcasted_iota(jnp.int32, (CHUNK, C), 1)
            packed_a, packed_b = comb_a[rows, :], comb_b[rows, :]

            def cell(shift):
                rows_e = pl.ds(PAD + r0 + shift, CHUNK)
                out = {name: ext[k, f, rows_e, :] for f, name in enumerate(names_a)}
                out.update({name: late[k, f, rows_e, :] for f, name in enumerate(names_b)})
                out["D"] = depth[rows_e, :]
                return out

            here, north, south = cell(0), cell(-1), cell(1)
            east, west = {}, {}
            for name, value in here.items():
                if name == "D":
                    edge = pltpu.roll(packed_a, C - 1 - 2 * ORIG * L, 1)
                elif name in names_a:
                    edge = pltpu.roll(packed_a, C - 1 - 2 * (k * ORIG + names_a.index(name)), 1)
                else:
                    edge = pltpu.roll(packed_b, C - 1 - 2 * (k * LATE + names_b.index(name)), 1)
                east[name] = jnp.where(lane == C - 1, edge, pltpu.roll(value, C - 1, 1))
                west[name] = jnp.where(lane == 0, edge, pltpu.roll(value, 1, 1))
            for item in (here, north, south, east, west):
                item["w"] = wet_at(item["D"], k)
            slope_w, step_w, flux_w = face(west, here)
            slope_e, step_e, flux_e = face(here, east)
            slope_n, step_n, flux_n = face(north, here)
            slope_s, step_s, flux_s = face(here, south)
            sx, sy = 0.5 * (slope_w + slope_e), 0.5 * (slope_n + slope_s)
            both = here["I"] + here["G"]
            for c, name in enumerate(("T", "S")):
                cross = sx * (0.5 * (step_w[c] + step_e[c])) + sy * (0.5 * (step_n[c] + step_s[c]))
                prod[k + 1, c, rows, :] = both * cross
                rhs[k, c, rows, :] = here[name] - (flux_e[c] - flux_w[c]) - (flux_s[c] - flux_n[c])
            prod[k + 1, 2, rows, :] = here["I"] * (sx * sx + sy * sy)

    def ends(step, carry):
        level_body(step * (L - 1))
        return carry

    def middles(k, carry):
        level_body(k)
        return carry

    lax.fori_loop(0, 2, ends, 0)
    prod_up = remote(PROD_UP, prod.at[1], prod.at[L + 1], {"gz": above})
    prod_down = remote(PROD_DOWN, prod.at[L], prod.at[0], {"gz": below})
    send(has_above, prod_up)
    send(has_below, prod_down)
    lax.fori_loop(1, L - 1, middles, 0)
    when(has_above, v_down.wait_recv)
    when(has_above, prod_down.wait_recv)
    when(has_below, prod_up.wait_recv)

    def assemble(step, carry):
        rows = pl.ds(pl.multiple_of(step * CHUNK, PAD), CHUNK)
        rows_e = pl.ds(pl.multiple_of(PAD + step * CHUNK, PAD), CHUNK)
        deep = depth[rows_e, :]
        wets = [wet_at(deep, k) for k in range(-1, L + 1)]
        prods = [prod[0, c, rows, :] for c in range(3)]
        flux = [None, None]
        for k in range(-1, L):
            gate = wets[k + 1] * wets[k + 2]
            nexts = [prod[k + 2, c, rows, :] for c in range(3)]
            for c in range(2):
                under = -0.5 * (nexts[c] + prods[c]) * gate
                if k >= 0:
                    rhs[k, c, rows, :] = (rhs[k, c, rows, :] - (under - flux[c])) * wets[k + 1]
                flux[c] = under
            cpl[k + 1, rows, :] = (vext[k + 1, rows, :] + 0.5 * (prods[2] + nexts[2])) * gate
            prods = nexts
        return carry

    lax.fori_loop(0, chunks, assemble, 0)

    upper = gz < nz // 2
    at_end = (gz == 0) | (gz == nz - 1)
    in_middle = (gz == nz // 2 - 1) | (gz == nz // 2)
    flip = jnp.where(upper, 0, 1)
    onward = jnp.where(upper, below, above)
    backward = jnp.where(upper, above, below)

    def level_at(j):
        return j + flip * (L - 1 - 2 * j)

    chain = remote(CHAIN, ch_out, ch_in, {"gz": onward})
    middle = remote(MIDDLE, ch_out, mid_in, {"gz": onward})
    back = remote(BACK, solved.at[level_at(0)], back_in, {"gz": backward})

    @pl.when(at_end)
    def _():
        ch_in[...] = jnp.zeros_like(ch_in)

    when(jnp.logical_not(at_end), chain.wait_recv)

    def eliminate(step, carry):
        rows = pl.ds(pl.multiple_of(step * CHUNK, PAD), CHUNK)
        weight, sums = ch_in[0, rows, :], [ch_in[1 + c, rows, :] for c in range(2)]
        for j in range(L):
            k = level_at(j)
            link = cpl[k + 1 - flip, rows, :]
            held = 1.0 + weight
            share = 1.0 / (held + link)
            factor = link * share
            right_side = [rhs[k, c, rows, :] + sums[c] for c in range(2)]
            if j == L - 1:
                last[0, rows, :] = held
                for c in range(2):
                    last[1 + c, rows, :] = right_side[c]
            weight = factor * held
            elim[j, 0, rows, :] = factor
            for c in range(2):
                elim[j, 1 + c, rows, :] = right_side[c] * share
                sums[c] = right_side[c] * factor
        ch_out[0, rows, :] = weight
        for c in range(2):
            ch_out[1 + c, rows, :] = sums[c]
        return carry

    lax.fori_loop(0, chunks, eliminate, 0)
    not_middle = jnp.logical_not(in_middle)
    not_end = jnp.logical_not(at_end)
    send(not_middle, chain)
    send(in_middle, middle)
    k_last = level_at(L - 1)

    @pl.when(in_middle)
    def _():
        middle.wait_recv()
        share = 1.0 / (last[0] + mid_in[0])
        for c in range(2):
            solved[k_last, c] = (last[1 + c] + mid_in[1 + c]) * share

    @pl.when(not_middle)
    def _():
        back.wait_recv()
        for c in range(2):
            solved[k_last, c] = elim[L - 1, 1 + c] + elim[L - 1, 0] * back_in[c]

    def substitute(step, carry):
        rows = pl.ds(pl.multiple_of(step * CHUNK, PAD), CHUNK)
        values = [solved[k_last, c, rows, :] for c in range(2)]
        for j in range(L - 2, -1, -1):
            k = level_at(j)
            factor = elim[j, 0, rows, :]
            for c in range(2):
                values[c] = elim[j, 1 + c, rows, :] + factor * values[c]
                solved[k, c, rows, :] = values[c]
        return carry

    lax.fori_loop(0, chunks, substitute, 0)
    send(not_end, back)
    stores = [load(8, solved.at[:, 0], t_out), load(9, solved.at[:, 1], s_out)]
    for item in stores:
        item.start()
    for item in stores:
        item.wait()
    for condition, item in sends:
        when(condition, item.wait_send)


def shards(*blocks):
    L, R, C = blocks[0].shape
    f32 = jnp.float32
    na, nb = L * ORIG + 1, L * LATE
    na_pad, nb_pad = -(-na // 8) * 8, -(-nb // 8) * 8
    assert 2 * na <= C and 2 * nb <= C and R % CHUNK == 0
    vmem = pltpu.VMEM
    slab = (R, C)
    scratch = [
        vmem((L, ORIG, R + 2 * PAD, C), f32),
        vmem((L, LATE, R + 2 * PAD, C), f32),
        vmem((R + 2 * PAD, C), f32),
        vmem((2, 2) + slab, f32),
        vmem((L + 1,) + slab, f32),
        vmem(slab, jnp.int32),
        vmem(slab, jnp.int32),
        vmem(slab, f32),
        vmem(slab, f32),
        vmem(slab, f32),
        vmem((2,) + slab, f32),
        vmem(slab, f32),
        vmem((2,) + slab, f32),
        vmem((2, na_pad, C), f32),
        vmem((2, na_pad, C), f32),
        vmem((2, nb_pad, C), f32),
        vmem((2, nb_pad, C), f32),
        vmem(slab, f32),
        vmem(slab, f32),
        vmem((L + 2, 3) + slab, f32),
        vmem((L, 2) + slab, f32),
        vmem((L + 1,) + slab, f32),
        vmem((L, 3) + slab, f32),
        vmem((3,) + slab, f32),
        vmem((3,) + slab, f32),
        vmem((3,) + slab, f32),
        vmem((3,) + slab, f32),
        vmem((L, 2) + slab, f32),
        vmem((2,) + slab, f32),
        pltpu.SemaphoreType.DMA((10,)),
        pltpu.SemaphoreType.DMA((17,)),
        pltpu.SemaphoreType.DMA((17,)),
    ]
    return pl.pallas_call(
        kernel,
        out_shape=[jax.ShapeDtypeStruct((L, R, C), f32)] * 2,
        in_specs=[pl.BlockSpec(memory_space=pl.ANY)] * 8,
        out_specs=[pl.BlockSpec(memory_space=pl.ANY)] * 2,
        scratch_shapes=scratch,
        compiler_params=pltpu.CompilerParams(
            collective_id=0, has_side_effects=True, vmem_limit_bytes=48 * 1024 * 1024
        ),
    )(*blocks)


def solution(mesh):
    field, flat = P("gz", "gy", "gx"), P("gy", "gx")
    return jax.shard_map(
        shards,
        mesh=mesh,
        in_specs=(field,) * 6 + (flat,) * 2,
        out_specs=(field, field),
        check_vma=False,
    )
```

profile of v0, /device:TPU:0, one launch (start us, length us, event | category | flops | bytes accessed | tf_op | source)
XLA Modules:
  0.0 42.3 jit_solution(10962489522400306386)
XLA Ops:
  0.6 0.0 copy-start
  0.6 1.0 %copy-done = f32[8,128,128]{2,1,0:T(8,128)S(1)} copy-done((f32[8,128,128]{2,1,0:T(8,128)S(1)}, f32[8,128,128]{2,1,0:T(8,128)}, u32[]{:S(2)}) %copy-start) | copy-done | bytes 524312
  1.7 0.0 copy-start.1
  1.7 1.0 %copy-done.1 = f32[8,128,128]{2,1,0:T(8,128)S(1)} copy-done((f32[8,128,128]{2,1,0:T(8,128)S(1)}, f32[8,128,128]{2,1,0:T(8,128)}, u32[]{:S(2)}) %copy-start.1) | copy-done | bytes 524312
  2.7 0.0 copy-start.2
  2.7 1.0 %copy-done.2 = f32[8,128,128]{2,1,0:T(8,128)S(1)} copy-done((f32[8,128,128]{2,1,0:T(8,128)S(1)}, f32[8,128,128]{2,1,0:T(8,128)}, u32[]{:S(2)}) %copy-start.2) | copy-done | bytes 524312
  3.8 0.0 copy-start.3
  3.8 1.0 %copy-done.3 = f32[8,128,128]{2,1,0:T(8,128)S(1)} copy-done((f32[8,128,128]{2,1,0:T(8,128)S(1)}, f32[8,128,128]{2,1,0:T(8,128)}, u32[]{:S(2)}) %copy-start.3) | copy-done | bytes 524312
  4.8 0.0 copy-start.4
  4.8 1.0 %copy-done.4 = f32[8,128,128]{2,1,0:T(8,128)S(1)} copy-done((f32[8,128,128]{2,1,0:T(8,128)S(1)}, f32[8,128,128]{2,1,0:T(8,128)}, u32[]{:S(2)}) %copy-start.4) | copy-done | bytes 524312
  5.8 0.0 copy-start.5
  5.8 1.0 %copy-done.5 = f32[8,128,128]{2,1,0:T(8,128)S(1)} copy-done((f32[8,128,128]{2,1,0:T(8,128)S(1)}, f32[8,128,128]{2,1,0:T(8,128)}, u32[]{:S(2)}) %copy-start.5) | copy-done | bytes 524312
  6.9 0.0 copy-start.6
  6.9 0.8 %copy-done.6 = s32[128,128]{1,0:T(8,128)S(1)} copy-done((s32[128,128]{1,0:T(8,128)S(1)}, s32[128,128]{1,0:T(8,128)}, u32[]{:S(2)}) %copy-start.6) | copy-done | bytes 65560
  7.7 0.0 copy-start.7
  7.7 0.8 %copy-done.7 = s32[128,128]{1,0:T(8,128)S(1)} copy-done((s32[128,128]{1,0:T(8,128)S(1)}, s32[128,128]{1,0:T(8,128)}, u32[]{:S(2)}) %copy-start.7) | copy-done | bytes 65560
  8.6 32.2 %shard_map.95 = (f32[8,128,128]{2,1,0:T(8,128)S(1)}, f32[8,128,128]{2,1,0:T(8,128)S(1)}) custom-call(f32[8,128,128]{2,1,0:T(8,128)S(1)} %copy-done, f32[8,128,128]{2,1,0:T(8,128)S(1)} %copy-done.1, f32[8,128,128]{2,1,0:T(8,128)S(1)} %copy-done.2, f32[8,128,128]{2,1,0:T(8,128)S(1)} %copy-done.3, f32[8,128,128]{2,1,0:T(8,128)S(1)} %copy-done.4, ...), custom_call_target="tpu_custom_call" | custom-call | tf_op jit(solution)/shard_map/pallas_call | solution.py:470
  40.7 0.8 %copy.12 = f32[8,128,128]{2,1,0:T(8,128)} copy(f32[8,128,128]{2,1,0:T(8,128)S(1)} %get-tuple-element.4) | data formatting | bytes 1048576
  41.5 0.8 %copy.13 = f32[8,128,128]{2,1,0:T(8,128)} copy(f32[8,128,128]{2,1,0:T(8,128)S(1)} %get-tuple-element.5) | data formatting | bytes 1048576
Async XLA Ops:
  0.6 1.0 %copy-start = (f32[8,128,128]{2,1,0:T(8,128)S(1)}, f32[8,128,128]{2,1,0:T(8,128)}, u32[]{:S(2)}) copy-start(f32[8,128,128]{2,1,0:T(8,128)} %t_in.1) | copy-start | bytes 1572868
  1.7 1.0 %copy-start.1 = (f32[8,128,128]{2,1,0:T(8,128)S(1)}, f32[8,128,128]{2,1,0:T(8,128)}, u32[]{:S(2)}) copy-start(f32[8,128,128]{2,1,0:T(8,128)} %s_in.1) | copy-start | bytes 1572868
  2.7 1.0 %copy-start.2 = (f32[8,128,128]{2,1,0:T(8,128)S(1)}, f32[8,128,128]{2,1,0:T(8,128)}, u32[]{:S(2)}) copy-start(f32[8,128,128]{2,1,0:T(8,128)} %n_in.1) | copy-start | bytes 1572868
  3.8 1.0 %copy-start.3 = (f32[8,128,128]{2,1,0:T(8,128)S(1)}, f32[8,128,128]{2,1,0:T(8,128)}, u32[]{:S(2)}) copy-start(f32[8,128,128]{2,1,0:T(8,128)} %v_in.1) | copy-start | bytes 1572868
  4.8 1.0 %copy-start.4 = (f32[8,128,128]{2,1,0:T(8,128)S(1)}, f32[8,128,128]{2,1,0:T(8,128)}, u32[]{:S(2)}) copy-start(f32[8,128,128]{2,1,0:T(8,128)} %i_in.1) | copy-start | bytes 1572868
  5.8 1.0 %copy-start.5 = (f32[8,128,128]{2,1,0:T(8,128)S(1)}, f32[8,128,128]{2,1,0:T(8,128)}, u32[]{:S(2)}) copy-start(f32[8,128,128]{2,1,0:T(8,128)} %g_in.1) | copy-start | bytes 1572868
  6.9 0.8 %copy-start.6 = (s32[128,128]{1,0:T(8,128)S(1)}, s32[128,128]{1,0:T(8,128)}, u32[]{:S(2)}) copy-start(s32[128,128]{1,0:T(8,128)} %flag_in.1) | copy-start | bytes 196612
  7.7 0.8 %copy-start.7 = (s32[128,128]{1,0:T(8,128)S(1)}, s32[128,128]{1,0:T(8,128)}, u32[]{:S(2)}) copy-start(s32[128,128]{1,0:T(8,128)} %count_in.1) | copy-start | bytes 196612
where the time goes:
time: 42.8 us; the launch traced here: 42.3 us
  Pallas kernels  32.2 us (75%)
  local copies, waits for them, and re-layouts  9.51 us (22%)
  between operations  0.66 us (2%)
    pallas_call x1, Pallas kernels, shards(): pl.pallas_call(kernel, out_shape=[jax.ShapeDtypeStruct((L, R, C), f32)] *...  32.2 us
    unnamed x18, local copies, waits for them, and re-layouts  9.51 us

commit v1 on v0

--- a/solution.py
+++ b/solution.py
@@ -50,7 +50,6 @@
     barrier = pltpu.get_barrier_semaphore()
     for target in ({"gx": right}, {"gx": left}, {"gy": later}, {"gy": earlier}, {"gz": below}, {"gz": above}):
         pl.semaphore_signal(barrier, inc=1, device_id=target, device_id_type=MESH)
-    pl.semaphore_wait(barrier, 6)
 
     def remote(number, src, dst, target):
         return pltpu.make_async_remote_copy(
@@ -97,6 +96,8 @@
     def _():
         pre[...] = jnp.zeros_like(pre)
 
+    pl.semaphore_wait(barrier, 6)
+
     @pl.when(gz == 0)
     def _():
         p_down.start()
@@ -111,14 +112,11 @@
     loads[6].wait()
     depth[inner, :] = jnp.where(flag[...] == 1, count[...], 0).astype(f32)
 
-    @pl.when(gz > 0)
+    @pl.when(has_above & has_below)
     def _():
         p_down.wait_recv()
-
-        @pl.when(has_below)
-        def _():
-            psend[...] = psend[...] + pre[...]
-            p_down.start()
+        psend[...] = psend[...] + pre[...]
+        p_down.start()
 
     loads[3].wait()
     loads[4].wait()
@@ -194,6 +192,7 @@
 
     when(has_above, z_down.wait_recv)
     when(has_below, z_up.wait_recv)
+    when(jnp.logical_not(has_below), p_down.wait_recv)
 
     def wet_at(deep, k):
         level = gz * L + k
@@ -474,7 +473,7 @@
         out_specs=[pl.BlockSpec(memory_space=pl.ANY)] * 2,
         scratch_shapes=scratch,
         compiler_params=pltpu.CompilerParams(
-            collective_id=0, has_side_effects=True, vmem_limit_bytes=48 * 1024 * 1024
+            collective_id=0, has_side_effects=True, vmem_limit_bytes=67043328
         ),
     )(*blocks)
 

time: 42.8 us -> 33.5 us (0.78)
  local copies, waits for them, and re-layouts: 9.51 us -> 2.73 us
  Pallas kernels: 32.2 us -> 29.9 us
    unnamed x18 -> x4, local copies, waits for them, and re-layouts: 9.51 us -> 2.73 us
    pallas_call x1, Pallas kernels: 32.2 us -> 29.9 us  [shards(): pl.pallas_call(kernel, out_shape=[jax.ShapeDtypeStruct((L, R, C), f32)] *...]
where the time goes in v1:
time: 33.5 us; the launch traced here: 33.3 us
  Pallas kernels  29.9 us (89%)
  local copies, waits for them, and re-layouts  2.73 us (8%)
  between operations  0.65 us (2%)
    pallas_call x1, Pallas kernels, shards(): pl.pallas_call(kernel, out_shape=[jax.ShapeDtypeStruct((L, R, C), f32)] *...  29.9 us
    unnamed x4, local copies, waits for them, and re-layouts  2.73 us

profile of v1, /device:TPU:0, one launch (start us, length us, event | category | flops | bytes accessed | tf_op | source)
XLA Modules:
  0.0 33.3 jit_solution(962819465746337928)
XLA Ops:
  0.6 29.9 %shard_map.95 = (f32[8,128,128]{2,1,0:T(8,128)}, f32[8,128,128]{2,1,0:T(8,128)}) custom-call(f32[8,128,128]{2,1,0:T(8,128)} %t_in.1, f32[8,128,128]{2,1,0:T(8,128)} %s_in.1, f32[8,128,128]{2,1,0:T(8,128)} %n_in.1, f32[8,128,128]{2,1,0:T(8,128)} %v_in.1, f32[8,128,128]{2,1,0:T(8,128)} %i_in.1, f32[8,128,128]{2,1,0:T(8,128)} %g_in.1, s32[128,128]{1,0:T(8,128)} %flag_in.1, ...), custom_call_target="tpu_custom_call" | custom-call | tf_op jit(solution)/shard_map/pallas_call | solution.py:469
  30.6 0.0 copy-start
  30.6 1.9 %copy.12 = f32[8,128,128]{2,1,0:T(8,128)} copy(f32[8,128,128]{2,1,0:T(8,128)} %get-tuple-element.4) | data formatting | bytes 1048576
  32.5 0.0 copy-done
  32.5 0.8 %copy.13 = f32[8,128,128]{2,1,0:T(8,128)} copy(f32[8,128,128]{2,1,0:T(8,128)S(1)} %copy-done) | data formatting | bytes 1048576
Async XLA Ops:
  30.6 1.9 %copy-start = (f32[8,128,128]{2,1,0:T(8,128)S(1)}, f32[8,128,128]{2,1,0:T(8,128)}, u32[]{:S(2)}) copy-start(f32[8,128,128]{2,1,0:T(8,128)} %get-tuple-element.5) | copy-start | bytes 1572868
